TPU v7x, 32 devices: a whole 2x2x4 slice. The times are simulated.
32 devices in a mesh: freq: 4 (over y, x), band: 8 (over z, core).
Axes of the slice: x: 2, y: 2, z: 4, core: 2. Of those that a mesh axis runs over, the one named last changes fastest.
Arguments:
- pair_density: bfloat16 [1024, 2, 8192], P(('freq', 'band')), may hold values from -6 to 6
- trial_vectors: bfloat16 [16, 2, 64, 8192], P('freq', None, None, 'band'), may hold values from -6 to 6
- frequency: float32 [16], P('freq'), may hold values from 0.05 to 20
- val_energy: float32 [32], replicated, may hold values from -3 to -0.1
- cond_energy: float32 [32], replicated, may hold values from 0.1 to 4
- pair_index: int32 [1024], P(('freq', 'band')), may hold values from 0 to 1023, each once
Outputs:
- images: float32 [16, 2, 64, 8192], P('freq', None, None, 'band')
- subspace: float32 [16, 2, 64, 64], P('freq')
Inputs may be any that keep to these rules, and one draw needn't show every extreme that they name: `pair_index`: every pair number 0 to 1023 appears exactly once.
All inputs are finite; a program needn't handle non-finite values.
Results may differ from a plain program's by a relative error of at most 0.0085.
Values may be sent and summed in bfloat16 or wider, within the bound.
A program may use at most 128 MiB of HBM per device.

v0:
```python
import math

import jax
import jax.numpy as jnp
from jax import lax
from jax.sharding import PartitionSpec as P


def local_weights(pair_index, frequency, val_energy, cond_energy, prefactor):
    cond_count = cond_energy.shape[0]
    val_count = val_energy.shape[0]
    cond_pick = jnp.sum(
        jnp.where(
            (pair_index % cond_count)[:, None] == jnp.arange(cond_count)[None, :],
            cond_energy[None, :],
            0.0,
        ),
        axis=1,
    )
    val_pick = jnp.sum(
        jnp.where(
            (pair_index // cond_count)[:, None] == jnp.arange(val_count)[None, :],
            val_energy[None, :],
            0.0,
        ),
        axis=1,
    )
    delta = cond_pick - val_pick
    ratio = delta[:, None] / (
        delta[:, None] * delta[:, None] + frequency[None, :] * frequency[None, :]
    )
    return (-4.0 * prefactor * ratio).astype(jnp.bfloat16)


def crossing_terms(density, vectors):
    products = jnp.einsum("pcg,fekg->fcekp", density, vectors, preferred_element_type=jnp.float32)
    return jnp.stack(
        [products[:, 0, 0] + products[:, 1, 1], products[:, 0, 1] - products[:, 1, 0]], 1
    )


def scale_terms(crossings, weights):
    factor = jnp.transpose(weights.astype(jnp.float32))[:, None, None, :]
    return (factor * crossings).astype(jnp.bfloat16)


def mix_terms(scaled):
    scaled_real = scaled[:, 0]
    scaled_imag = scaled[:, 1]
    return jnp.stack(
        [jnp.stack([scaled_real, -scaled_imag], 1), jnp.stack([scaled_imag, scaled_real], 1)], 1
    )


def image_terms(density, mixed):
    return jnp.einsum("pcg,fdckp->fdkg", density, mixed, preferred_element_type=jnp.float32)


def shards(pair_density, trial_vectors, frequency, val_energy, cond_energy, pair_index):
    groups = lax.axis_size("freq")
    members = lax.axis_size("band")
    pair_count = pair_density.shape[0] * groups * members
    grid_count = trial_vectors.shape[3] * members
    prefactor = 1.0 / math.sqrt(2.0 * grid_count * pair_count)
    regrouped = lax.all_to_all(pair_density, "band", split_axis=2, concat_axis=0, tiled=True)
    grouped = lax.all_gather(regrouped, "freq", axis=0, tiled=True)
    all_index = lax.all_gather(pair_index, ("freq", "band"), axis=0, tiled=True)
    crossings = crossing_terms(grouped, trial_vectors)
    summed = lax.psum(crossings, "band")
    all_weights = local_weights(all_index, frequency, val_energy, cond_energy, prefactor)
    scaled = scale_terms(summed, all_weights)
    images = image_terms(grouped, mix_terms(scaled))
    vectors = trial_vectors.astype(jnp.float32)
    highest = lax.Precision.HIGHEST
    real_part = jnp.einsum(
        "fkg,flg->fkl", vectors[:, 0], images[:, 0], precision=highest
    ) + jnp.einsum("fkg,flg->fkl", vectors[:, 1], images[:, 1], precision=highest)
    imag_part = jnp.einsum(
        "fkg,flg->fkl", vectors[:, 0], images[:, 1], precision=highest
    ) - jnp.einsum("fkg,flg->fkl", vectors[:, 1], images[:, 0], precision=highest)
    partial_value = jnp.stack([real_part, imag_part], 1) / grid_count
    subspace = lax.psum(partial_value, "band")
    return (images, subspace)


def solution(mesh):
    return jax.shard_map(
        shards,
        mesh=mesh,
        in_specs=(
            P(("freq", "band"), None, None),
            P("freq", None, None, "band"),
            P("freq"),
            P(),
            P(),
            P(("freq", "band")),
        ),
        out_specs=(P("freq", None, None, "band"), P("freq", None, None, None)),
        check_vma=False,
    )
```

profile of v0, /device:TPU:1, one launch (start us, length us, event | category | flops | bytes accessed | tf_op | source)
XLA Modules:
  0.0 267.3 jit_solution(9058504637230988360)
XLA Ops:
  7.2 10.8 %copy.31 = bf16[32,2,8192]{0,1,2:T(2,128)(2,1)} copy(bf16[32,2,8192]{2,1,0:T(2,128)(2,1)} %param.6) | data formatting | bytes 2097152 | tf_op args[0]
  18.0 7.0 %reshape.101 = bf16[8,2,32768]{2,1,0:T(2,128)(2,1)S(1)} reshape(bf16[8192,2,32]{2,1,0:T(2,128)(2,1)} %bitcast.76) | data formatting | bytes 2097152
  24.9 31.7 %all_to_all.18 = bf16[8,2,32768]{2,1,0:T(2,128)(2,1)S(1)} all-to-all(bf16[8,2,32768]{2,1,0:T(2,128)(2,1)S(1)} %reshape.101), channel_id=1, replica_groups=mesh['freq'=4,'band'=8] {'band'}, dimensions={0} | all-to-all | bytes 2097152 | tf_op jit(solution)/shard_map/all_to_all | solution.py:65
  56.6 4.5 %reshape.102 = bf16[8192,2,32]{2,1,0:T(2,128)(2,1)} reshape(bf16[8,2,32768]{2,1,0:T(2,128)(2,1)S(1)} %all_to_all.18) | data formatting | bytes 2097152
  61.1 10.5 %copy.32 = bf16[32,2,8,1024]{3,0,2,1:T(8,128)(2,1)} copy(bf16[32,2,8,1024]{0,1,3,2:T(2,128)(2,1)} %bitcast.75) | data formatting | bytes 2097152 | tf_op jit(solution)/shard_map/all_to_all | solution.py:65
  71.7 51.8 %all-gather.2.cloned.1.call-done = bf16[1024,2,1024]{2,0,1:T(8,128)(2,1)} async-done(((bf16[256,2,1024]{2,0,1:T(8,128)(2,1)}), bf16[1024,2,1024]{2,0,1:T(8,128)(2,1)}) %all-gather.2.cloned.1.call-update) | async-done | bytes 4194320 | tf_op jit(solution)/shard_map/all_gather | solution.py:66
  123.5 4.6 %fusion.4 = f32[4,2,2,64,1024]{4,3,1,2,0:T(8,128)S(1)} fusion(bf16[1024,2,1024]{2,0,1:T(8,128)(2,1)} %all-gather.2.cloned.1.call-done, bf16[4,2,64,1024]{3,2,1,0:T(8,128)(2,1)S(1)} %copy-done.1), kind=kOutput, calls=%fused_computation.4 | convolution fusion | flops 2147483648 | bytes 9437184 | tf_op jit(solution)/shard_map/pcg,fekg->fcekp/dot_general | solution.py:36
  128.0 0.1 fusion.15
  128.3 1.5 pad_maximum_fusion
  129.9 0.6 copy-done.5
  130.5 0.2 dynamic-update-slice
  130.7 39.0 %all-reduce = s32[1024]{0:T(1024)S(1)} all-reduce(s32[1024]{0:T(1024)S(1)} %dynamic-update-slice), channel_id=1, replica_groups=mesh['freq'=4,'band'=8] {'freq','band'}, use_global_device_ids=true, to_apply=%add | all-reduce | flops 1024 | bytes 8192
  169.9 24.5 %all-reduce.4.cloned.1.call-done = f32[4,2,64,1024]{3,2,0,1:T(8,128)} async-done(((f32[4,2,64,1024]{3,2,0,1:T(8,128)}), f32[4,2,64,1024]{3,2,0,1:T(8,128)}) %all-reduce.4.cloned.1.call-update) | async-done | bytes 2097168 | tf_op jit(solution)/shard_map/psum | solution.py:69
  194.4 1.8 multiply_convert_fusion
  196.4 0.2 maximum_bitcast_fusion
  196.6 1.9 copy-done.4
  198.4 2.3 fusion.8
  200.8 0.6 fusion.20
  201.4 0.6 fusion.19
  202.1 0.6 fusion.13
  202.7 0.6 fusion.14
  203.4 0.7 maximum_multiply_fusion
  204.1 54.9 %all-reduce.6.cloned.1.call-done = f32[4,2,64,64]{2,3,0,1:T(8,128)} async-done(((f32[4,2,64,64]{2,3,0,1:T(8,128)}), f32[4,2,64,64]{2,3,0,1:T(8,128)}) %all-reduce.6.cloned.1.call-update) | async-done | bytes 131088 | tf_op jit(solution)/shard_map/psum | solution.py:82
  259.0 1.8 copy.38
  (26 shorter events, 0.7 us)
Async XLA Ops:
  7.2 116.3 %all-gather.2.cloned.1.call-start = ((), (), s32[]{:S(2)}) async-start(), calls=%async_computation.1 | async-start | bytes 5242880 | tf_op jit(solution)/shard_map/all_gather | solution.py:66
  61.1 62.4 %copy-start.1 = (bf16[4,2,64,1024]{3,2,1,0:T(8,128)(2,1)S(1)}, bf16[4,2,64,1024]{3,2,1,0:T(8,128)(2,1)}, u32[]{:S(2)}) copy-start(bf16[4,2,64,1024]{3,2,1,0:T(8,128)(2,1)} %param.7) | copy-start | bytes 3145732
  71.6 122.8 %all-reduce.4.cloned.1.call-start = ((), (), s32[]{:S(2)}) async-start(), calls=%async_computation.2 | async-start | bytes 4194304 | tf_op jit(solution)/shard_map/psum | solution.py:69
  129.8 0.7 copy-start.5
  129.8 0.7 copy-start.6
  129.8 39.9 %copy-start.2 = (f32[32]{0:T(128)S(1)}, f32[32]{0:T(128)}, u32[]{:S(2)}) copy-start(f32[32]{0:T(128)} %param.9) | copy-start | bytes 388
  129.8 39.9 %copy-start.3 = (f32[32]{0:T(128)S(1)}, f32[32]{0:T(128)}, u32[]{:S(2)}) copy-start(f32[32]{0:T(128)} %param.10) | copy-start | bytes 388
  129.8 129.2 %all-reduce.6.cloned.1.call-start = ((), (), s32[]{:S(2)}) async-start(), calls=%async_computation.3 | async-start | bytes 524288 | tf_op jit(solution)/shard_map/psum | solution.py:82
  196.3 2.2 copy-start.4
  200.8 1.9 copy-start
Sparse Core Ops, SparseCore 0:
  71.7 51.6 all-gather.1
  129.9 64.4 all-reduce.3
  204.2 54.7 all-reduce.5
where the time goes:
time: 271 us; the launch traced here: 267 us
  waiting for transfers between devices  131 us (48%)
  blocking collectives  70.7 us (26%)
  local copies, waits for them, and re-layouts  37.2 us (14%)
  between operations  13.9 us (5%)
  matrix products  9.4 us (3%)
  other arithmetic  4.8 us (2%)
    psum x1, waiting for transfers between devices, shards(): subspace = lax.psum(partial_value, 'band')  54.9 us
    all_gather x1, waiting for transfers between devices, shards(): grouped = lax.all_gather(regrouped, 'freq', axis=0, tiled=True)  51.8 us
    unnamed x1, blocking collectives  39 us
    all_to_all x1, blocking collectives, shards(): lax.all_to_all(pair_density, 'band', split_axis=2, concat_axis=0, tiled=T...  31.7 us
    unnamed x20, local copies, waits for them, and re-layouts  26.7 us
    psum x1, waiting for transfers between devices, shards(): summed = lax.psum(crossings, 'band')  24.5 us
    all_to_all x1, local copies, waits for them, and re-layouts, shards(): lax.all_to_all(pair_density, 'band', split_axis=2, concat_axis=0, tiled=T...  10.5 us
  transfers between devices with their start and end apart: 3, of which 3 were waited for; matrix products, arithmetic and copies ran while one was open for 0% of the time, Pallas kernels for 0%

commit v1 on v0

v1 whole, which is shorter than its diff:
```python
import functools
import math

import jax
import jax.numpy as jnp
from jax import lax
from jax.experimental import pallas as pl
from jax.experimental.pallas import tpu as pltpu
from jax.sharding import PartitionSpec as P

MESH = pl.DeviceIdType.MESH
F32 = jnp.float32
BF16 = jnp.bfloat16


def local_delta(pair_index, val_energy, cond_energy):
    cond_count = cond_energy.shape[0]
    val_count = val_energy.shape[0]
    cond_pick = jnp.sum(
        jnp.where(
            (pair_index % cond_count)[:, None] == jnp.arange(cond_count)[None, :],
            cond_energy[None, :],
            0.0,
        ),
        axis=1,
    )
    val_pick = jnp.sum(
        jnp.where(
            (pair_index // cond_count)[:, None] == jnp.arange(val_count)[None, :],
            val_energy[None, :],
            0.0,
        ),
        axis=1,
    )
    return cond_pick - val_pick


def kernel(
    groups, members, freqs, vecs, rows, grid_here, prefactor, inv_grid,
    dens, trial, freq_row, delta_own,
    images, sub,
    held, mix, deltas, part_out, part_in, own, ring_out, ring_in, scaled, acc,
    sem_as, sem_ar, sem_fs, sem_fr, sem_ds, sem_dr, sem_es, sem_er,
    sem_ps, sem_pr, sem_rs, sem_rr, sem_gs, sem_gr, sem_hs, sem_hr,
):
    f = lax.axis_index("freq")
    b = lax.axis_index("band")
    chips = members // 2
    chunks = members // 2
    zc = b // 2
    core = b % 2
    width = freqs * 2 * vecs
    chunk_rows = 2 * groups * rows
    partner = zc * 2 + (1 - core)

    def remote(src, dst, send, recv, freq_id, band_id):
        return pltpu.make_async_remote_copy(
            src_ref=src, dst_ref=dst, send_sem=send, recv_sem=recv,
            device_id=(freq_id, band_id), device_id_type=MESH,
        )

    barrier = pltpu.get_barrier_semaphore()
    for s in range(1, members):
        pl.semaphore_signal(barrier, inc=1, device_id=(f, (b + s) % members), device_id_type=MESH)
    for s in range(1, groups):
        pl.semaphore_signal(barrier, inc=1, device_id=((f + s) % groups, b), device_id_type=MESH)
    pl.semaphore_wait(barrier, members + groups - 2)

    sends = []

    def go(copy):
        copy.start()
        sends.append(copy)

    mine = pltpu.make_async_copy(dens.at[b], held.at[b, f], sem_ar.at[b])
    mine.start()
    for s in range(1, members):
        to = (b + s) % members
        go(remote(dens.at[to], held.at[b, f], sem_as.at[s], sem_ar.at[b], f, to))
    mine_delta = pltpu.make_async_copy(delta_own, deltas.at[f, b], sem_dr.at[b])
    mine_delta.start()
    for s in range(1, members):
        to = (b + s) % members
        go(remote(delta_own, deltas.at[f, b], sem_ds.at[s], sem_dr.at[b], f, to))

    for q in range(freqs):
        lo, hi = q * 2 * vecs, (q * 2 + 1) * vecs
        top = trial[lo : lo + vecs, :]
        low = trial[hi : hi + vecs, :]
        mix[lo : lo + vecs, 0:grid_here] = top
        mix[lo : lo + vecs, grid_here:] = low
        mix[hi : hi + vecs, 0:grid_here] = low
        mix[hi : hi + vecs, grid_here:] = -top

    for j in range(members):
        pltpu.make_async_copy(delta_own, deltas.at[f, j], sem_dr.at[j]).wait()
    for s in range(1, groups):
        go(remote(deltas.at[f], deltas.at[f], sem_es.at[s], sem_er.at[s], (f + s) % groups, b))

    for j in range(members):
        pltpu.make_async_copy(dens.at[0], held.at[j, f], sem_ar.at[j]).wait()
        for s in range(1, groups):
            go(remote(held.at[j, f], held.at[j, f], sem_fs.at[j, s], sem_fr.at[j, s], (f + s) % groups, b))

    for s in range(1, groups):
        src = (f + groups - s) % groups
        remote(deltas.at[src], deltas.at[src], sem_es.at[s], sem_er.at[s], src, b).wait_recv()

    def weights(column):
        ratio = column / (column * column + freq_row[...] * freq_row[...])
        return (-4.0 * prefactor * ratio).astype(BF16).astype(F32)

    def block_delta(g, j):
        return jnp.transpose(deltas[g, j])[0:rows, 0:1]

    def cross(j):
        for m in (2 * j, 2 * j + 1):
            for s in range(1, groups):
                src = (f + groups - s) % groups
                remote(held.at[m, src], held.at[m, src], sem_fs.at[m, s], sem_fr.at[m, s], src, b).wait_recv()
        block = held[2 * j : 2 * j + 2].reshape(chunk_rows, 2 * grid_here)
        own[...] = lax.dot_general(
            block, mix[...], (((1,), (1,)), ((), ())), preferred_element_type=F32
        ).reshape(2, chips, chunk_rows // members, width)
        part_out[j] = own[1 - core].astype(BF16)
        go(remote(part_out.at[j], part_in.at[j], sem_ps.at[j], sem_pr.at[j], f, partner))
        remote(part_out.at[j], part_in.at[j], sem_ps.at[j], sem_pr.at[j], f, partner).wait_recv()
        total = own[core] + part_in[j].astype(F32)
        ring_out[j] = total.astype(BF16)
        for s in range(1, chips):
            to = (zc + s) % chips
            go(remote(ring_out.at[j, to], ring_in.at[j, s], sem_rs.at[j, s], sem_rr.at[j, s], f, to * 2 + core))

    def scale(j):
        total = ring_out[j, zc].astype(F32)
        for s in range(1, chips):
            src = (zc + chips - s) % chips
            remote(ring_out.at[j, zc], ring_in.at[j, s], sem_rs.at[j, s], sem_rr.at[j, s], f, src * 2 + core).wait_recv()
            total = total + ring_in[j, s].astype(F32)
        q = core * chips + zc
        column = block_delta(q % groups, 2 * j + q // groups)
        scaled[j, core, zc] = (weights(column) * total).astype(BF16)
        for s in range(1, chips):
            to = (zc + s) % chips
            go(remote(scaled.at[j, core, zc], scaled.at[j, core, zc], sem_gs.at[j, s], sem_gr.at[j, s], f, to * 2 + core))

    def share(j):
        for s in range(1, chips):
            src = (zc + chips - s) % chips
            remote(scaled.at[j, core, src], scaled.at[j, core, src], sem_gs.at[j, s], sem_gr.at[j, s], f, src * 2 + core).wait_recv()
        go(remote(scaled.at[j, core], scaled.at[j, core], sem_hs.at[j], sem_hr.at[j], f, partner))

    def image(j):
        remote(scaled.at[j, 1 - core], scaled.at[j, 1 - core], sem_hs.at[j], sem_hr.at[j], f, partner).wait_recv()
        flat = scaled[j].reshape(chunk_rows, width)
        flat32 = flat.astype(F32)
        lane = lax.broadcasted_iota(jnp.int32, (1, 2 * vecs), 1)
        sign = jnp.where(lane < vecs, -1.0, 1.0)
        turned = jnp.concatenate(
            [
                pltpu.roll(flat32[:, q * 2 * vecs : (q + 1) * 2 * vecs], vecs, 1) * sign
                for q in range(freqs)
            ],
            axis=1,
        ).astype(BF16)
        over_rows = (((0,), (0,)), ((), ()))
        real = held[2 * j : 2 * j + 2, :, :, 0:grid_here].reshape(chunk_rows, grid_here)
        imag = held[2 * j : 2 * j + 2, :, :, grid_here:].reshape(chunk_rows, grid_here)
        term = lax.dot_general(flat, real, over_rows, preferred_element_type=F32) + lax.dot_general(
            turned, imag, over_rows, preferred_element_type=F32
        )
        column = jnp.concatenate(
            [block_delta(q % groups, 2 * j + q // groups) for q in range(2 * groups)], axis=0
        )
        crossing = (flat32 / weights(column)).astype(BF16)
        for q in range(freqs):
            lo, hi = q * 2 * vecs, (q + 1) * 2 * vecs
            square = lax.dot_general(
                crossing[:, lo:hi], flat[:, lo:hi], over_rows, preferred_element_type=F32
            )
            if j == 0:
                acc[q] = square
            else:
                acc[q] = acc[q] + square
        if j == 0:
            images[...] = term
        else:
            images[...] = images[...] + term

    for t in range(chunks + 2):
        if t < chunks:
            cross(t)
        if 0 <= t - 1 < chunks:
            scale(t - 1)
        if 0 <= t - 2 < chunks:
            share(t - 2)
            image(t - 2)

    for q in range(freqs):
        square = acc[q]
        lo, hi = q * 2 * vecs, (q * 2 + 1) * vecs
        sub[lo : lo + vecs, :] = (square[0:vecs, 0:vecs] + square[vecs:, vecs:]) * inv_grid
        sub[hi : hi + vecs, :] = (square[0:vecs, vecs:] - square[vecs:, 0:vecs]) * inv_grid

    for copy in sends:
        copy.wait_send()


def shards(pair_density, trial_vectors, frequency, val_energy, cond_energy, pair_index):
    groups = lax.axis_size("freq")
    members = lax.axis_size("band")
    rows = pair_density.shape[0]
    freqs, _, vecs, grid_here = trial_vectors.shape
    pair_count = rows * groups * members
    grid_count = grid_here * members
    prefactor = 1.0 / math.sqrt(2.0 * grid_count * pair_count)
    width = freqs * 2 * vecs
    chips = members // 2
    chunks = members // 2
    slot = 2 * groups * rows // members
    dens = jnp.transpose(
        pair_density.reshape(rows, 2, members, grid_here), (2, 0, 1, 3)
    ).reshape(members, rows, 2 * grid_here)
    trial = trial_vectors.reshape(width, grid_here)
    freq_row = jnp.repeat(frequency, 2 * vecs)[None, :]
    delta = local_delta(pair_index, val_energy, cond_energy)
    delta_own = jnp.broadcast_to(jnp.pad(delta, (0, 128 - rows))[None, :], (8, 128))
    dma = pltpu.SemaphoreType.DMA
    vmem = pl.BlockSpec(memory_space=pltpu.VMEM)
    images, sub = pl.pallas_call(
        functools.partial(
            kernel, groups, members, freqs, vecs, rows, grid_here, prefactor, 1.0 / grid_count
        ),
        out_shape=(
            jax.ShapeDtypeStruct((width, grid_here), F32),
            jax.ShapeDtypeStruct((width, vecs), F32),
        ),
        in_specs=[vmem] * 4,
        out_specs=(vmem, vmem),
        scratch_shapes=[
            pltpu.VMEM((members, groups, rows, 2 * grid_here), BF16),
            pltpu.VMEM((width, 2 * grid_here), BF16),
            pltpu.VMEM((groups, members, 8, 128), F32),
            pltpu.VMEM((chunks, chips, slot, width), BF16),
            pltpu.VMEM((chunks, chips, slot, width), BF16),
            pltpu.VMEM((2, chips, slot, width), F32),
            pltpu.VMEM((chunks, chips, slot, width), BF16),
            pltpu.VMEM((chunks, chips, slot, width), BF16),
            pltpu.VMEM((chunks, 2, chips, slot, width), BF16),
            pltpu.VMEM((freqs, 2 * vecs, 2 * vecs), F32),
            dma((members,)), dma((members,)),
            dma((members, groups)), dma((members, groups)),
            dma((members,)), dma((members,)),
            dma((groups,)), dma((groups,)),
            dma((chunks,)), dma((chunks,)),
            dma((chunks, chips)), dma((chunks, chips)),
            dma((chunks, chips)), dma((chunks, chips)),
            dma((chunks,)), dma((chunks,)),
        ],
        compiler_params=pltpu.CompilerParams(
            collective_id=0, has_side_effects=True, vmem_limit_bytes=56 * 1024 * 1024
        ),
    )(dens, trial, freq_row, delta_own)
    return (
        images.reshape(freqs, 2, vecs, grid_here),
        sub.reshape(freqs, 2, vecs, vecs),
    )


def solution(mesh):
    return jax.shard_map(
        shards,
        mesh=mesh,
        in_specs=(
            P(("freq", "band"), None, None),
            P("freq", None, None, "band"),
            P("freq"),
            P(),
            P(),
            P(("freq", "band")),
        ),
        out_specs=(P("freq", None, None, "band"), P("freq", None, None, None)),
        check_vma=False,
    )
```

time: 271 us -> 109 us (0.40); the launches traced: 267 us -> 109 us
  waiting for transfers between devices: 131 us -> 0 us
  Pallas kernels: 0 us -> 97 us
  blocking collectives: 70.7 us -> 0 us
  local copies, waits for them, and re-layouts: 37.2 us -> 9.37 us
  between operations: 13.9 us -> 0.67 us
  matrix products: 9.4 us -> 0 us
  other arithmetic: 4.8 us -> 1.52 us
    pallas_call x0 -> x1, Pallas kernels: none -> 97 us  [shards(): pl.pallas_call(functools.partial(kernel, groups, members, freqs, vecs, ro...]
    psum x2 -> x0, waiting for transfers between devices: 79.4 us -> none  [the longest x1 54.9 us: shards(): subspace = lax.psum(partial_value, 'band')]
    all_gather x1 -> x0, waiting for transfers between devices: 51.8 us -> none  [shards(): grouped = lax.all_gather(regrouped, 'freq', axis=0, tiled=True)]
    unnamed x1 -> x0, blocking collectives: 39 us -> none
    all_to_all x1 -> x0, blocking collectives: 31.7 us -> none  [shards(): lax.all_to_all(pair_density, 'band', split_axis=2, concat_axis=0, tiled=T...]
    unnamed x20 -> x4, local copies, waits for them, and re-layouts: 26.7 us -> 3.91 us
    all_to_all x1 -> x0, local copies, waits for them, and re-layouts: 10.5 us -> none  [shards(): lax.all_to_all(pair_density, 'band', split_axis=2, concat_axis=0, tiled=T...]
    dot_general x6 -> x0, matrix products: 9.4 us -> none  [the longest x1 4.55 us: crossing_terms(): jnp.einsum('pcg,fekg->fcekp', density, vectors, preferred_element_type=jn...]
  transfers between devices with their start and end apart: 3 -> 0, of which waited for: 3 -> 0; matrix products, arithmetic and copies ran while one was open for 0% -> 0% of each run, Pallas kernels for 0% -> 0%
where the time goes in v1:
time: 109 us
  Pallas kernels  97 us (89%)
  local copies, waits for them, and re-layouts  9.37 us (9%)
  other arithmetic  1.52 us (1%)
    pallas_call x1, Pallas kernels, shards(): pl.pallas_call(functools.partial(kernel, groups, members, freqs, vecs, ro...  97 us
    unnamed x4, local copies, waits for them, and re-layouts  3.91 us

profile of v1, /device:TPU:1, one launch (start us, length us, event | category | flops | bytes accessed | tf_op | source)
XLA Modules:
  0.0 108.6 jit_solution(8295111966831947337)
XLA Ops:
  0.6 0.7 and_select_fusion
  1.3 0.9 select_reduce_fusion
  2.2 1.3 %broadcast_in_dim.33 = f32[4,128]{1,0:T(4,128)} broadcast(f32[4]{0:T(128)} %param.8), dimensions={0} | broadcast | bytes 2064 | tf_op jit(solution)/shard_map/broadcast_in_dim | solution.py:225
  3.5 0.6 broadcast_in_dim.37.delta_own
  4.1 1.9 %copy.12 = bf16[32,1,8,2,1024]{4,3,1,0,2:T(2,128)(2,1)S(1)} copy(bf16[32,1,8,2,1024]{4,3,2,1,0:T(2,128)(2,1)} %bitcast.14) | data formatting | bytes 2097152 | tf_op jit(solution)/shard_map/reshape | solution.py:222
  6.0 1.6 %reshape.25.dens = bf16[8,32,2048]{2,1,0:T(8,128)(2,1)} reshape(bf16[8,32,2,1024]{3,2,1,0:T(2,128)(2,1)S(1)} %bitcast.11) | data formatting | bytes 2097152 | tf_op jit(solution)/shard_map/reshape | solution.py:223
  7.6 97.0 %shard_map.77 = (f32[512,1024]{1,0:T(8,128)}, f32[512,64]{1,0:T(8,128)}) custom-call(bf16[8,32,2048]{2,1,0:T(8,128)(2,1)} %reshape.25.dens, bf16[512,1024]{1,0:T(8,128)(2,1)} %bitcast.13, f32[1,512]{1,0:T(1,128)} %bitcast.16, f32[8,128]{1,0:T(8,128)} %broadcast_in_dim.37.delta_own), custom_call_target="tpu_custom_call" | custom-call | tf_op jit(solution)/shard_map/pallas_call | solution.py:230
  104.7 0.0 copy-start
  104.7 3.2 %copy.15 = f32[4,2,64,1024]{3,2,1,0:T(8,128)} copy(f32[4,2,64,1024]{3,2,1,0:T(8,128)} %bitcast.12) | data formatting | bytes 4194304
  107.9 0.0 copy-done
  107.9 0.7 copy.16
  (2 shorter events, 0.0 us)
Async XLA Ops:
  104.7 3.2 %copy-start = (f32[512,64]{1,0:T(8,128)S(1)}, f32[512,64]{1,0:T(8,128)}, u32[]{:S(2)}) copy-start(f32[512,64]{1,0:T(8,128)} %get-tuple-element.5) | copy-start | bytes 393220

commit v2 on v1

--- a/solution.py
+++ b/solution.py
@@ -36,21 +36,22 @@
 
 
 def kernel(
-    groups, members, freqs, vecs, rows, grid_here, prefactor, inv_grid,
+    groups, members, chunks, freqs, vecs, rows, grid_here, prefactor, inv_grid,
     dens, trial, freq_row, delta_own,
     images, sub,
-    held, mix, deltas, part_out, part_in, own, ring_out, ring_in, scaled, acc,
+    held, mix, deltas, cols, part_out, part_in, own, ring_out, ring_in, scaled, acc,
     sem_as, sem_ar, sem_fs, sem_fr, sem_ds, sem_dr, sem_es, sem_er,
     sem_ps, sem_pr, sem_rs, sem_rr, sem_gs, sem_gr, sem_hs, sem_hr,
 ):
     f = lax.axis_index("freq")
     b = lax.axis_index("band")
     chips = members // 2
-    chunks = members // 2
+    piece = rows // chunks
     zc = b // 2
     core = b % 2
     width = freqs * 2 * vecs
-    chunk_rows = 2 * groups * rows
+    chunk_rows = groups * members * piece
+    slot = groups * piece
     partner = zc * 2 + (1 - core)
 
     def remote(src, dst, send, recv, freq_id, band_id):
@@ -72,16 +73,17 @@
         copy.start()
         sends.append(copy)
 
-    mine = pltpu.make_async_copy(dens.at[b], held.at[b, f], sem_ar.at[b])
-    mine.start()
-    for s in range(1, members):
-        to = (b + s) % members
-        go(remote(dens.at[to], held.at[b, f], sem_as.at[s], sem_ar.at[b], f, to))
-    mine_delta = pltpu.make_async_copy(delta_own, deltas.at[f, b], sem_dr.at[b])
-    mine_delta.start()
-    for s in range(1, members):
-        to = (b + s) % members
-        go(remote(delta_own, deltas.at[f, b], sem_ds.at[s], sem_dr.at[b], f, to))
+    for c in range(chunks):
+        pltpu.make_async_copy(dens.at[c, b], held.at[c, f, b], sem_ar.at[c, b]).start()
+        for s in range(1, members):
+            to = (b + s) % members
+            go(remote(dens.at[c, to], held.at[c, f, b], sem_as.at[c, s], sem_ar.at[c, b], f, to))
+        if c == 0:
+            mine_delta = pltpu.make_async_copy(delta_own, deltas.at[f, b], sem_dr.at[b])
+            mine_delta.start()
+            for s in range(1, members):
+                to = (b + s) % members
+                go(remote(delta_own, deltas.at[f, b], sem_ds.at[s], sem_dr.at[b], f, to))
 
     for q in range(freqs):
         lo, hi = q * 2 * vecs, (q * 2 + 1) * vecs
@@ -97,28 +99,63 @@
     for s in range(1, groups):
         go(remote(deltas.at[f], deltas.at[f], sem_es.at[s], sem_er.at[s], (f + s) % groups, b))
 
-    for j in range(members):
-        pltpu.make_async_copy(dens.at[0], held.at[j, f], sem_ar.at[j]).wait()
+    square_groups = groups == 4
+    xx, yy = f % 2, f // 2
+    fx, fy = yy * 2 + (1 - xx), (1 - yy) * 2 + xx
+    fd = (1 - yy) * 2 + (1 - xx)
+    half = members // 2
+
+    def whole(c, g, lane, peer):
+        return remote(held.at[c, g], held.at[c, g], sem_fs.at[c, lane], sem_fr.at[c, lane], peer, b)
+
+    def part(c, g, first, lane, peer):
+        ref = held.at[c, g, first : first + half]
+        return remote(ref, ref, sem_fs.at[c, lane], sem_fr.at[c, lane], peer, b)
+
+    def spread(c):
+        for j in range(members):
+            pltpu.make_async_copy(dens.at[c, 0], held.at[c, f, j], sem_ar.at[c, j]).wait()
+        if square_groups:
+            go(whole(c, f, 0, fx))
+            go(whole(c, f, 1, fy))
+        else:
+            for s in range(1, groups):
+                go(whole(c, f, s, (f + s) % groups))
+
+    def relay(c):
+        if square_groups:
+            whole(c, fx, 0, fx).wait_recv()
+            go(part(c, fx, 0, 2, fy))
+            whole(c, fy, 1, fy).wait_recv()
+            go(part(c, fy, half, 3, fx))
+
+    def arrive(c):
+        if square_groups:
+            part(c, fd, 0, 2, fy).wait_recv()
+            part(c, fd, half, 3, fx).wait_recv()
+        else:
+            for s in range(1, groups):
+                src = (f + groups - s) % groups
+                whole(c, src, s, src).wait_recv()
+
+    def columns():
         for s in range(1, groups):
-            go(remote(held.at[j, f], held.at[j, f], sem_fs.at[j, s], sem_fr.at[j, s], (f + s) % groups, b))
-
-    for s in range(1, groups):
-        src = (f + groups - s) % groups
-        remote(deltas.at[src], deltas.at[src], sem_es.at[s], sem_er.at[s], src, b).wait_recv()
+            src = (f + groups - s) % groups
+            remote(deltas.at[src], deltas.at[src], sem_es.at[s], sem_er.at[s], src, b).wait_recv()
+        for g in range(groups):
+            for j in range(members):
+                turned = jnp.transpose(deltas[g, j])
+                at = (g * members + j) * piece
+                for c in range(chunks):
+                    cols[c, at : at + piece, :] = turned[c * piece : (c + 1) * piece, :]
 
     def weights(column):
         ratio = column / (column * column + freq_row[...] * freq_row[...])
         return (-4.0 * prefactor * ratio).astype(BF16).astype(F32)
 
-    def block_delta(g, j):
-        return jnp.transpose(deltas[g, j])[0:rows, 0:1]
-
     def cross(j):
-        for m in (2 * j, 2 * j + 1):
-            for s in range(1, groups):
-                src = (f + groups - s) % groups
-                remote(held.at[m, src], held.at[m, src], sem_fs.at[m, s], sem_fr.at[m, s], src, b).wait_recv()
-        block = held[2 * j : 2 * j + 2].reshape(chunk_rows, 2 * grid_here)
+        arrive(j)
+        block = held[j].reshape(chunk_rows, 2 * grid_here)
         own[...] = lax.dot_general(
             block, mix[...], (((1,), (1,)), ((), ())), preferred_element_type=F32
         ).reshape(2, chips, chunk_rows // members, width)
@@ -138,7 +175,7 @@
             remote(ring_out.at[j, zc], ring_in.at[j, s], sem_rs.at[j, s], sem_rr.at[j, s], f, src * 2 + core).wait_recv()
             total = total + ring_in[j, s].astype(F32)
         q = core * chips + zc
-        column = block_delta(q % groups, 2 * j + q // groups)
+        column = cols[j, pl.ds(pl.multiple_of(q * slot, 8), slot), 0:1]
         scaled[j, core, zc] = (weights(column) * total).astype(BF16)
         for s in range(1, chips):
             to = (zc + s) % chips
@@ -164,14 +201,12 @@
             axis=1,
         ).astype(BF16)
         over_rows = (((0,), (0,)), ((), ()))
-        real = held[2 * j : 2 * j + 2, :, :, 0:grid_here].reshape(chunk_rows, grid_here)
-        imag = held[2 * j : 2 * j + 2, :, :, grid_here:].reshape(chunk_rows, grid_here)
+        real = held[j, :, :, :, 0:grid_here].reshape(chunk_rows, grid_here)
+        imag = held[j, :, :, :, grid_here:].reshape(chunk_rows, grid_here)
         term = lax.dot_general(flat, real, over_rows, preferred_element_type=F32) + lax.dot_general(
             turned, imag, over_rows, preferred_element_type=F32
         )
-        column = jnp.concatenate(
-            [block_delta(q % groups, 2 * j + q // groups) for q in range(2 * groups)], axis=0
-        )
+        column = cols[j, :, 0:1]
         crossing = (flat32 / weights(column)).astype(BF16)
         for q in range(freqs):
             lo, hi = q * 2 * vecs, (q + 1) * 2 * vecs
@@ -187,8 +222,13 @@
         else:
             images[...] = images[...] + term
 
+    spread(0)
+    columns()
     for t in range(chunks + 2):
+        if t + 1 < chunks:
+            spread(t + 1)
         if t < chunks:
+            relay(t)
             cross(t)
         if 0 <= t - 1 < chunks:
             scale(t - 1)
@@ -216,11 +256,12 @@
     prefactor = 1.0 / math.sqrt(2.0 * grid_count * pair_count)
     width = freqs * 2 * vecs
     chips = members // 2
-    chunks = members // 2
-    slot = 2 * groups * rows // members
+    chunks = rows // 8
+    piece = rows // chunks
+    slot = groups * piece
     dens = jnp.transpose(
-        pair_density.reshape(rows, 2, members, grid_here), (2, 0, 1, 3)
-    ).reshape(members, rows, 2 * grid_here)
+        pair_density.reshape(chunks, piece, 2, members, grid_here), (0, 3, 1, 2, 4)
+    ).reshape(chunks, members, piece, 2 * grid_here)
     trial = trial_vectors.reshape(width, grid_here)
     freq_row = jnp.repeat(frequency, 2 * vecs)[None, :]
     delta = local_delta(pair_index, val_energy, cond_energy)
@@ -229,7 +270,7 @@
     vmem = pl.BlockSpec(memory_space=pltpu.VMEM)
     images, sub = pl.pallas_call(
         functools.partial(
-            kernel, groups, members, freqs, vecs, rows, grid_here, prefactor, 1.0 / grid_count
+            kernel, groups, members, chunks, freqs, vecs, rows, grid_here, prefactor, 1.0 / grid_count
         ),
         out_shape=(
             jax.ShapeDtypeStruct((width, grid_here), F32),
@@ -238,9 +279,10 @@
         in_specs=[vmem] * 4,
         out_specs=(vmem, vmem),
         scratch_shapes=[
-            pltpu.VMEM((members, groups, rows, 2 * grid_here), BF16),
+            pltpu.VMEM((chunks, groups, members, piece, 2 * grid_here), BF16),
             pltpu.VMEM((width, 2 * grid_here), BF16),
             pltpu.VMEM((groups, members, 8, 128), F32),
+            pltpu.VMEM((chunks, members * slot, 8), F32),
             pltpu.VMEM((chunks, chips, slot, width), BF16),
             pltpu.VMEM((chunks, chips, slot, width), BF16),
             pltpu.VMEM((2, chips, slot, width), F32),
@@ -248,8 +290,8 @@
             pltpu.VMEM((chunks, chips, slot, width), BF16),
             pltpu.VMEM((chunks, 2, chips, slot, width), BF16),
             pltpu.VMEM((freqs, 2 * vecs, 2 * vecs), F32),
-            dma((members,)), dma((members,)),
-            dma((members, groups)), dma((members, groups)),
+            dma((chunks, members)), dma((chunks, members)),
+            dma((chunks, groups)), dma((chunks, groups)),
             dma((members,)), dma((members,)),
             dma((groups,)), dma((groups,)),
             dma((chunks,)), dma((chunks,)),

time: 109 us -> 99 us (0.908)
  Pallas kernels: 97 us -> 87.4 us
    pallas_call x1, Pallas kernels: 97 us -> 87.4 us  [shards(): pl.pallas_call(functools.partial(kernel, groups, members, chunks, freqs,...]
where the time goes in v2:
time: 99 us; the launch traced here: 98.7 us
  Pallas kernels  87.4 us (88%)
  local copies, waits for them, and re-layouts  9.2 us (9%)
  other arithmetic  1.52 us (2%)
    pallas_call x1, Pallas kernels, shards(): pl.pallas_call(functools.partial(kernel, groups, members, chunks, freqs,...  87.4 us
    unnamed x4, local copies, waits for them, and re-layouts  3.91 us
    reshape x2, local copies, waits for them, and re-layouts, shards(): pair_density.reshape(chunks, piece, 2, members, grid_here)  3.38 us

profile of v2, /device:TPU:1, one launch (start us, length us, event | category | flops | bytes accessed | tf_op | source)
XLA Modules:
  0.0 98.7 jit_solution(2098327369065711854)
XLA Ops:
  0.6 0.7 and_select_fusion
  1.3 0.9 select_reduce_fusion
  2.2 1.3 %broadcast_in_dim.33 = f32[4,128]{1,0:T(4,128)} broadcast(f32[4]{0:T(128)} %param.8), dimensions={0} | broadcast | bytes 2064 | tf_op jit(solution)/shard_map/broadcast_in_dim | solution.py:266
  3.5 0.6 broadcast_in_dim.37.delta_own
  4.1 1.8 %reshape.24 = bf16[4,8,2,8,1024]{4,3,2,1,0:T(8,128)(2,1)S(1)} reshape(bf16[32,2,8192]{2,1,0:T(2,128)(2,1)} %param.6) | data formatting | bytes 2097152 | tf_op jit(solution)/shard_map/reshape | solution.py:263
  5.9 1.6 %copy.9 = bf16[4,8,2,8,1024]{4,1,2,3,0:T(8,128)(2,1)} copy(bf16[4,8,2,8,1024]{4,3,2,1,0:T(8,128)(2,1)S(1)} %reshape.24) | data formatting | bytes 2097152 | tf_op jit(solution)/shard_map/reshape | solution.py:263
  7.5 87.4 %shard_map.77 = (f32[512,1024]{1,0:T(8,128)}, f32[512,64]{1,0:T(8,128)}) custom-call(bf16[4,8,8,2048]{3,2,1,0:T(8,128)(2,1)} %bitcast.7, bf16[512,1024]{1,0:T(8,128)(2,1)} %bitcast.9, f32[1,512]{1,0:T(1,128)} %bitcast.11, f32[8,128]{1,0:T(8,128)} %broadcast_in_dim.37.delta_own), custom_call_target="tpu_custom_call" | custom-call | tf_op jit(solution)/shard_map/pallas_call | solution.py:271
  94.8 0.0 copy-start
  94.8 3.2 %copy.12 = f32[4,2,64,1024]{3,2,1,0:T(8,128)} copy(f32[4,2,64,1024]{3,2,1,0:T(8,128)} %bitcast.8) | data formatting | bytes 4194304
  98.0 0.0 copy-done
  98.0 0.7 copy.13
  (2 shorter events, 0.0 us)
Async XLA Ops:
  94.8 3.2 %copy-start = (f32[512,64]{1,0:T(8,128)S(1)}, f32[512,64]{1,0:T(8,128)}, u32[]{:S(2)}) copy-start(f32[512,64]{1,0:T(8,128)} %get-tuple-element.5) | copy-start | bytes 393220

commit v3 on v2

--- a/solution.py
+++ b/solution.py
@@ -13,33 +13,11 @@
 BF16 = jnp.bfloat16
 
 
-def local_delta(pair_index, val_energy, cond_energy):
-    cond_count = cond_energy.shape[0]
-    val_count = val_energy.shape[0]
-    cond_pick = jnp.sum(
-        jnp.where(
-            (pair_index % cond_count)[:, None] == jnp.arange(cond_count)[None, :],
-            cond_energy[None, :],
-            0.0,
-        ),
-        axis=1,
-    )
-    val_pick = jnp.sum(
-        jnp.where(
-            (pair_index // cond_count)[:, None] == jnp.arange(val_count)[None, :],
-            val_energy[None, :],
-            0.0,
-        ),
-        axis=1,
-    )
-    return cond_pick - val_pick
-
-
 def kernel(
     groups, members, chunks, freqs, vecs, rows, grid_here, prefactor, inv_grid,
-    dens, trial, freq_row, delta_own,
+    dens, trial, frequency, val_energy, cond_energy, pair_index,
     images, sub,
-    held, mix, deltas, cols, part_out, part_in, own, ring_out, ring_in, scaled, acc,
+    held, mix, delta_own, freq_row, deltas, cols, part_out, part_in, own, ring_out, ring_in, scaled, acc,
     sem_as, sem_ar, sem_fs, sem_fr, sem_ds, sem_dr, sem_es, sem_er,
     sem_ps, sem_pr, sem_rs, sem_rr, sem_gs, sem_gr, sem_hs, sem_hr,
 ):
@@ -75,15 +53,33 @@
 
     for c in range(chunks):
         pltpu.make_async_copy(dens.at[c, b], held.at[c, f, b], sem_ar.at[c, b]).start()
-        for s in range(1, members):
-            to = (b + s) % members
-            go(remote(dens.at[c, to], held.at[c, f, b], sem_as.at[c, s], sem_ar.at[c, b], f, to))
-        if c == 0:
-            mine_delta = pltpu.make_async_copy(delta_own, deltas.at[f, b], sem_dr.at[b])
-            mine_delta.start()
-            for s in range(1, members):
-                to = (b + s) % members
-                go(remote(delta_own, deltas.at[f, b], sem_ds.at[s], sem_dr.at[b], f, to))
+        go(remote(dens.at[c, partner], held.at[c, f, b], sem_as.at[c, 0], sem_ar.at[c, b], f, partner))
+    def exchange(c):
+        for r in range(1, chips):
+            for k in range(2):
+                to = (zc + r) % chips * 2 + (core + k) % 2
+                go(remote(dens.at[c, to], held.at[c, f, b], sem_as.at[c, 2 * r + k], sem_ar.at[c, b], f, to))
+
+    cond_count = cond_energy.shape[0]
+    val_count = val_energy.shape[0]
+    index = pair_index[...]
+    rest_index = index
+    val_pick = jnp.full(index.shape, val_energy[0], F32)
+    for v in range(1, val_count):
+        above = index >= v * cond_count
+        val_pick = jnp.where(above, val_energy[v], val_pick)
+        rest_index = jnp.where(above, index - v * cond_count, rest_index)
+    cond_pick = jnp.full(index.shape, cond_energy[0], F32)
+    for v in range(1, cond_count):
+        cond_pick = jnp.where(rest_index == v, cond_energy[v], cond_pick)
+    delta_own[...] = jnp.ones_like(delta_own)
+    delta_own[0:1, 0:rows] = cond_pick - val_pick
+    for q in range(freqs):
+        freq_row[:, q * 2 * vecs : (q + 1) * 2 * vecs] = jnp.full((1, 2 * vecs), frequency[q], F32)
+    pltpu.make_async_copy(delta_own, deltas.at[f, b], sem_dr.at[b]).start()
+    for s in range(1, members):
+        to = (b + s) % members
+        go(remote(delta_own, deltas.at[f, b], sem_ds.at[s], sem_dr.at[b], f, to))
 
     for q in range(freqs):
         lo, hi = q * 2 * vecs, (q * 2 + 1) * vecs
@@ -94,49 +90,62 @@
         mix[hi : hi + vecs, 0:grid_here] = low
         mix[hi : hi + vecs, grid_here:] = -top
 
-    for j in range(members):
-        pltpu.make_async_copy(delta_own, deltas.at[f, j], sem_dr.at[j]).wait()
-    for s in range(1, groups):
-        go(remote(deltas.at[f], deltas.at[f], sem_es.at[s], sem_er.at[s], (f + s) % groups, b))
-
     square_groups = groups == 4
     xx, yy = f % 2, f // 2
     fx, fy = yy * 2 + (1 - xx), (1 - yy) * 2 + xx
     fd = (1 - yy) * 2 + (1 - xx)
-    half = members // 2
+
+    def piece_copy(c, g, z, lane, peer):
+        ref = held.at[c, g, pl.ds(2 * z, 2)]
+        return remote(ref, ref, sem_fs.at[c, lane, z], sem_fr.at[c, lane, z], peer, b)
 
     def whole(c, g, lane, peer):
-        return remote(held.at[c, g], held.at[c, g], sem_fs.at[c, lane], sem_fr.at[c, lane], peer, b)
-
-    def part(c, g, first, lane, peer):
-        ref = held.at[c, g, first : first + half]
-        return remote(ref, ref, sem_fs.at[c, lane], sem_fr.at[c, lane], peer, b)
-
-    def spread(c):
-        for j in range(members):
-            pltpu.make_async_copy(dens.at[c, 0], held.at[c, f, j], sem_ar.at[c, j]).wait()
-        if square_groups:
-            go(whole(c, f, 0, fx))
-            go(whole(c, f, 1, fy))
-        else:
+        return remote(held.at[c, g], held.at[c, g], sem_fs.at[c, lane, 0], sem_fr.at[c, lane, 0], peer, b)
+
+    def spread(c, offsets):
+        for r in offsets:
+            z = (zc + r) % chips
+            for k in range(2):
+                j = z * 2 + k
+                pltpu.make_async_copy(dens.at[c, 0], held.at[c, f, j], sem_ar.at[c, j]).wait()
+            if square_groups:
+                go(piece_copy(c, f, z, 0, fx))
+                go(piece_copy(c, f, z, 1, fy))
+        if not square_groups and offsets[-1] == chips - 1:
             for s in range(1, groups):
                 go(whole(c, f, s, (f + s) % groups))
 
     def relay(c):
         if square_groups:
-            whole(c, fx, 0, fx).wait_recv()
-            go(part(c, fx, 0, 2, fy))
-            whole(c, fy, 1, fy).wait_recv()
-            go(part(c, fy, half, 3, fx))
+            for r in range(chips):
+                z = (zc + r) % chips
+                if r % 2 == 0:
+                    piece_copy(c, fx, z, 0, fx).wait_recv()
+                    go(piece_copy(c, fx, z, 2, fy))
+                else:
+                    piece_copy(c, fy, z, 1, fy).wait_recv()
+                    go(piece_copy(c, fy, z, 3, fx))
 
     def arrive(c):
         if square_groups:
-            part(c, fd, 0, 2, fy).wait_recv()
-            part(c, fd, half, 3, fx).wait_recv()
+            for r in range(chips):
+                z = (zc + r) % chips
+                if r % 2 == 0:
+                    piece_copy(c, fy, z, 1, fy).wait_recv()
+                    piece_copy(c, fd, z, 2, fy).wait_recv()
+                else:
+                    piece_copy(c, fx, z, 0, fx).wait_recv()
+                    piece_copy(c, fd, z, 3, fx).wait_recv()
         else:
             for s in range(1, groups):
                 src = (f + groups - s) % groups
                 whole(c, src, s, src).wait_recv()
+
+    def pass_deltas():
+        for j in range(members):
+            pltpu.make_async_copy(delta_own, deltas.at[f, j], sem_dr.at[j]).wait()
+        for s in range(1, groups):
+            go(remote(deltas.at[f], deltas.at[f], sem_es.at[s], sem_er.at[s], (f + s) % groups, b))
 
     def columns():
         for s in range(1, groups):
@@ -222,19 +231,27 @@
         else:
             images[...] = images[...] + term
 
-    spread(0)
-    columns()
-    for t in range(chunks + 2):
-        if t + 1 < chunks:
-            spread(t + 1)
+    exchange(0)
+    for c in range(chunks):
+        spread(c, (0,))
+    exchange(1)
+    pass_deltas()
+    for t in range(chunks + 4):
         if t < chunks:
-            relay(t)
-            cross(t)
+            spread(t, range(1, chips))
+        if t + 2 < chunks:
+            exchange(t + 2)
+        if t == 0:
+            columns()
         if 0 <= t - 1 < chunks:
-            scale(t - 1)
+            relay(t - 1)
+        if 0 <= t - 3 < chunks:
+            scale(t - 3)
         if 0 <= t - 2 < chunks:
-            share(t - 2)
-            image(t - 2)
+            cross(t - 2)
+        if 0 <= t - 4 < chunks:
+            share(t - 4)
+            image(t - 4)
 
     for q in range(freqs):
         square = acc[q]
@@ -263,11 +280,9 @@
         pair_density.reshape(chunks, piece, 2, members, grid_here), (0, 3, 1, 2, 4)
     ).reshape(chunks, members, piece, 2 * grid_here)
     trial = trial_vectors.reshape(width, grid_here)
-    freq_row = jnp.repeat(frequency, 2 * vecs)[None, :]
-    delta = local_delta(pair_index, val_energy, cond_energy)
-    delta_own = jnp.broadcast_to(jnp.pad(delta, (0, 128 - rows))[None, :], (8, 128))
     dma = pltpu.SemaphoreType.DMA
     vmem = pl.BlockSpec(memory_space=pltpu.VMEM)
+    smem = pl.BlockSpec(memory_space=pltpu.SMEM)
     images, sub = pl.pallas_call(
         functools.partial(
             kernel, groups, members, chunks, freqs, vecs, rows, grid_here, prefactor, 1.0 / grid_count
@@ -276,11 +291,13 @@
             jax.ShapeDtypeStruct((width, grid_here), F32),
             jax.ShapeDtypeStruct((width, vecs), F32),
         ),
-        in_specs=[vmem] * 4,
+        in_specs=[vmem] * 2 + [smem] * 3 + [vmem],
         out_specs=(vmem, vmem),
         scratch_shapes=[
             pltpu.VMEM((chunks, groups, members, piece, 2 * grid_here), BF16),
             pltpu.VMEM((width, 2 * grid_here), BF16),
+            pltpu.VMEM((8, 128), F32),
+            pltpu.VMEM((1, width), F32),
             pltpu.VMEM((groups, members, 8, 128), F32),
             pltpu.VMEM((chunks, members * slot, 8), F32),
             pltpu.VMEM((chunks, chips, slot, width), BF16),
@@ -291,7 +308,7 @@
             pltpu.VMEM((chunks, 2, chips, slot, width), BF16),
             pltpu.VMEM((freqs, 2 * vecs, 2 * vecs), F32),
             dma((chunks, members)), dma((chunks, members)),
-            dma((chunks, groups)), dma((chunks, groups)),
+            dma((chunks, groups, chips)), dma((chunks, groups, chips)),
             dma((members,)), dma((members,)),
             dma((groups,)), dma((groups,)),
             dma((chunks,)), dma((chunks,)),
@@ -302,7 +319,7 @@
         compiler_params=pltpu.CompilerParams(
             collective_id=0, has_side_effects=True, vmem_limit_bytes=56 * 1024 * 1024
         ),
-    )(dens, trial, freq_row, delta_own)
+    )(dens, trial, frequency, val_energy, cond_energy, pair_index[None, :])
     return (
         images.reshape(freqs, 2, vecs, grid_here),
         sub.reshape(freqs, 2, vecs, vecs),

time: 99 us -> 79.7 us (0.81)
  Pallas kernels: 87.4 us -> 71.6 us
  local copies, waits for them, and re-layouts: 9.2 us -> 7.29 us
  other arithmetic: 1.52 us -> 0 us
    pallas_call x1, Pallas kernels: 87.4 us -> 71.6 us  [shards(): pl.pallas_call(functools.partial(kernel, groups, members, chunks, freqs,...]
    broadcast_in_dim x2 -> x0, local copies, waits for them, and re-layouts: 1.91 us -> none  [the longest x1 1.32 us: shards(): freq_row = jnp.repeat(frequency, 2 * vecs)[None, :]]
where the time goes in v3:
time: 79.7 us; the launch traced here: 79.5 us
  Pallas kernels  71.6 us (90%)
  local copies, waits for them, and re-layouts  7.29 us (9%)
    pallas_call x1, Pallas kernels, shards(): pl.pallas_call(functools.partial(kernel, groups, members, chunks, freqs,...  71.6 us
    unnamed x4, local copies, waits for them, and re-layouts  3.91 us
    reshape x2, local copies, waits for them, and re-layouts, shards(): pair_density.reshape(chunks, piece, 2, members, grid_here)  3.38 us

profile of v3, /device:TPU:1, one launch (start us, length us, event | category | flops | bytes accessed | tf_op | source)
XLA Modules:
  0.0 79.5 jit_solution(7314175633535143795)
XLA Ops:
  0.6 1.8 %reshape.19 = bf16[4,8,2,8,1024]{4,3,2,1,0:T(8,128)(2,1)S(1)} reshape(bf16[32,2,8192]{2,1,0:T(2,128)(2,1)} %param.6) | data formatting | bytes 2097152 | tf_op jit(solution)/shard_map/reshape | solution.py:280
  2.5 1.6 %copy.8 = bf16[4,8,2,8,1024]{4,1,2,3,0:T(8,128)(2,1)} copy(bf16[4,8,2,8,1024]{4,3,2,1,0:T(8,128)(2,1)S(1)} %reshape.19) | data formatting | bytes 2097152 | tf_op jit(solution)/shard_map/reshape | solution.py:280
  4.0 71.6 %shard_map.77 = (f32[512,1024]{1,0:T(8,128)}, f32[512,64]{1,0:T(8,128)}) custom-call(bf16[4,8,8,2048]{3,2,1,0:T(8,128)(2,1)} %bitcast.7, bf16[512,1024]{1,0:T(8,128)(2,1)} %bitcast.9, f32[4]{0:T(128)} %frequency.1, f32[32]{0:T(128)} %val_energy.1, f32[32]{0:T(128)} %cond_energy.1, s32[1,32]{1,0:T(1,128)} %bitcast.11), custom_call_target="tpu_custom_call" | custom-call | tf_op jit(solution)/shard_map/pallas_call | solution.py:286
  75.6 0.0 copy-start
  75.6 3.2 %copy.11 = f32[4,2,64,1024]{3,2,1,0:T(8,128)} copy(f32[4,2,64,1024]{3,2,1,0:T(8,128)} %bitcast.8) | data formatting | bytes 4194304
  78.8 0.0 copy-done
  78.8 0.7 copy.12
Async XLA Ops:
  75.6 3.2 %copy-start = (f32[512,64]{1,0:T(8,128)S(1)}, f32[512,64]{1,0:T(8,128)}, u32[]{:S(2)}) copy-start(f32[512,64]{1,0:T(8,128)} %get-tuple-element.5) | copy-start | bytes 393220

commit v4 on v3

--- a/solution.py
+++ b/solution.py
@@ -45,6 +45,9 @@
         pl.semaphore_signal(barrier, inc=1, device_id=((f + s) % groups, b), device_id_type=MESH)
     pl.semaphore_wait(barrier, members + groups - 2)
 
+    def waves(c, to):
+        return dens.at[c, :, :, pl.ds(pl.multiple_of(to * grid_here, 128), grid_here)]
+
     sends = []
 
     def go(copy):
@@ -52,13 +55,13 @@
         sends.append(copy)
 
     for c in range(chunks):
-        pltpu.make_async_copy(dens.at[c, b], held.at[c, f, b], sem_ar.at[c, b]).start()
-        go(remote(dens.at[c, partner], held.at[c, f, b], sem_as.at[c, 0], sem_ar.at[c, b], f, partner))
+        pltpu.make_async_copy(waves(c, b), held.at[c, f, b], sem_ar.at[c, b]).start()
+        go(remote(waves(c, partner), held.at[c, f, b], sem_as.at[c, 0], sem_ar.at[c, b], f, partner))
     def exchange(c):
         for r in range(1, chips):
             for k in range(2):
                 to = (zc + r) % chips * 2 + (core + k) % 2
-                go(remote(dens.at[c, to], held.at[c, f, b], sem_as.at[c, 2 * r + k], sem_ar.at[c, b], f, to))
+                go(remote(waves(c, to), held.at[c, f, b], sem_as.at[c, 2 * r + k], sem_ar.at[c, b], f, to))
 
     cond_count = cond_energy.shape[0]
     val_count = val_energy.shape[0]
@@ -107,7 +110,7 @@
             z = (zc + r) % chips
             for k in range(2):
                 j = z * 2 + k
-                pltpu.make_async_copy(dens.at[c, 0], held.at[c, f, j], sem_ar.at[c, j]).wait()
+                pltpu.make_async_copy(waves(c, 0), held.at[c, f, j], sem_ar.at[c, j]).wait()
             if square_groups:
                 go(piece_copy(c, f, z, 0, fx))
                 go(piece_copy(c, f, z, 1, fy))
@@ -164,9 +167,12 @@
 
     def cross(j):
         arrive(j)
-        block = held[j].reshape(chunk_rows, 2 * grid_here)
-        own[...] = lax.dot_general(
-            block, mix[...], (((1,), (1,)), ((), ())), preferred_element_type=F32
+        over_grid = (((1,), (1,)), ((), ()))
+        real = held[j, :, :, 0].reshape(chunk_rows, grid_here)
+        imag = held[j, :, :, 1].reshape(chunk_rows, grid_here)
+        own[...] = (
+            lax.dot_general(real, mix[:, 0:grid_here], over_grid, preferred_element_type=F32)
+            + lax.dot_general(imag, mix[:, grid_here:], over_grid, preferred_element_type=F32)
         ).reshape(2, chips, chunk_rows // members, width)
         part_out[j] = own[1 - core].astype(BF16)
         go(remote(part_out.at[j], part_in.at[j], sem_ps.at[j], sem_pr.at[j], f, partner))
@@ -210,8 +216,8 @@
             axis=1,
         ).astype(BF16)
         over_rows = (((0,), (0,)), ((), ()))
-        real = held[j, :, :, :, 0:grid_here].reshape(chunk_rows, grid_here)
-        imag = held[j, :, :, :, grid_here:].reshape(chunk_rows, grid_here)
+        real = held[j, :, :, 0].reshape(chunk_rows, grid_here)
+        imag = held[j, :, :, 1].reshape(chunk_rows, grid_here)
         term = lax.dot_general(flat, real, over_rows, preferred_element_type=F32) + lax.dot_general(
             turned, imag, over_rows, preferred_element_type=F32
         )
@@ -234,13 +240,12 @@
     exchange(0)
     for c in range(chunks):
         spread(c, (0,))
-    exchange(1)
     pass_deltas()
     for t in range(chunks + 4):
+        if t + 1 < chunks:
+            exchange(t + 1)
         if t < chunks:
             spread(t, range(1, chips))
-        if t + 2 < chunks:
-            exchange(t + 2)
         if t == 0:
             columns()
         if 0 <= t - 1 < chunks:
@@ -277,8 +282,8 @@
     piece = rows // chunks
     slot = groups * piece
     dens = jnp.transpose(
-        pair_density.reshape(chunks, piece, 2, members, grid_here), (0, 3, 1, 2, 4)
-    ).reshape(chunks, members, piece, 2 * grid_here)
+        pair_density.reshape(chunks, piece, 2, grid_count), (0, 2, 1, 3)
+    )
     trial = trial_vectors.reshape(width, grid_here)
     dma = pltpu.SemaphoreType.DMA
     vmem = pl.BlockSpec(memory_space=pltpu.VMEM)
@@ -294,7 +299,7 @@
         in_specs=[vmem] * 2 + [smem] * 3 + [vmem],
         out_specs=(vmem, vmem),
         scratch_shapes=[
-            pltpu.VMEM((chunks, groups, members, piece, 2 * grid_here), BF16),
+            pltpu.VMEM((chunks, groups, members, 2, piece, grid_here), BF16),
             pltpu.VMEM((width, 2 * grid_here), BF16),
             pltpu.VMEM((8, 128), F32),
             pltpu.VMEM((1, width), F32),

time: 79.7 us -> 78.6 us (0.986)
  Pallas kernels: 71.6 us -> 70.5 us
    pallas_call x1, Pallas kernels: 71.6 us -> 70.5 us  [shards(): pl.pallas_call(functools.partial(kernel, groups, members, chunks, freqs,...]
    reshape x2 -> x1, local copies, waits for them, and re-layouts: 3.38 us -> 2.78 us  [shards(): pair_density.reshape(chunks, piece, 2, grid_count)]
where the time goes in v4:
time: 78.6 us; the launch traced here: 77.8 us
  Pallas kernels  70.5 us (90%)
  local copies, waits for them, and re-layouts  6.68 us (8%)
    pallas_call x1, Pallas kernels, shards(): pl.pallas_call(functools.partial(kernel, groups, members, chunks, freqs,...  70.5 us
    unnamed x4, local copies, waits for them, and re-layouts  3.91 us
    reshape x1, local copies, waits for them, and re-layouts, shards(): pair_density.reshape(chunks, piece, 2, grid_count)  2.78 us

profile of v4, /device:TPU:1, one launch (start us, length us, event | category | flops | bytes accessed | tf_op | source)
XLA Modules:
  0.0 77.8 jit_solution(7312525875353971030)
XLA Ops:
  0.6 2.8 %copy.13 = bf16[4,8,2,8192]{3,1,2,0:T(8,128)(2,1)} copy(bf16[4,8,2,8192]{3,2,1,0:T(2,128)(2,1)} %bitcast.11) | data formatting | bytes 2097152 | tf_op jit(solution)/shard_map/reshape | solution.py:285
  3.4 70.5 %shard_map.77 = (f32[512,1024]{1,0:T(8,128)}, f32[512,64]{1,0:T(8,128)}) custom-call(bf16[4,2,8,8192]{3,2,1,0:T(8,128)(2,1)} %bitcast.8, bf16[512,1024]{1,0:T(8,128)(2,1)} %bitcast.10, f32[4]{0:T(128)} %frequency.1, f32[32]{0:T(128)} %val_energy.1, f32[32]{0:T(128)} %cond_energy.1, s32[1,32]{1,0:T(1,128)} %bitcast.13), custom_call_target="tpu_custom_call" | custom-call | tf_op jit(solution)/shard_map/pallas_call | solution.py:291
  73.9 0.0 copy-start
  73.9 3.2 %copy.16 = f32[4,2,64,1024]{3,2,1,0:T(8,128)} copy(f32[4,2,64,1024]{3,2,1,0:T(8,128)} %bitcast.9) | data formatting | bytes 4194304
  77.1 0.0 copy-done
  77.1 0.7 copy.17
Async XLA Ops:
  73.9 3.2 %copy-start = (f32[512,64]{1,0:T(8,128)S(1)}, f32[512,64]{1,0:T(8,128)}, u32[]{:S(2)}) copy-start(f32[512,64]{1,0:T(8,128)} %get-tuple-element.5) | copy-start | bytes 393220
